TPU v7x, 32 devices: a whole 2x2x4 slice. The times are simulated.
32 devices in a mesh: row: 8 (over z, core), col: 4 (over y, x).
Axes of the slice: x: 2, y: 2, z: 4, core: 2. Of those that a mesh axis runs over, the one named last changes fastest.
Arguments:
- images: bfloat16 [512, 12, 12, 272], P(('row', 'col')), may hold values from -20 to 20
- expand_weight: bfloat16 [2, 272, 1632], replicated, may hold values from -0.375 to 0.375
- depth_kernel: float32 [2, 25, 1632], replicated, may hold values from -1.25 to 1.25
- squeeze_weight: float32 [2, 1632, 68], replicated, may hold values from -0.15625 to 0.15625
- squeeze_bias: float32 [2, 68], replicated, may hold values from -3 to 3
- excite_weight: float32 [2, 68, 1632], replicated, may hold values from -0.75 to 0.75
- excite_bias: float32 [2, 1632], replicated, may hold values from -4 to 4
- project_weight: bfloat16 [2, 1632, 272], replicated, may hold values from -0.15625 to 0.15625
- mid_gain: float32 [2, 2, 1632], replicated, may hold values from 0.5 to 1.5
- mid_bias: float32 [2, 2, 1632], replicated, may hold values from -3 to 3
- out_gain: float32 [2, 272], replicated, may hold values from 0.5 to 1.5
- out_bias: float32 [2, 272], replicated, may hold values from -3 to 3
- mid_mean: float32 [2, 2, 1632], replicated, may hold values from -4 to 4
- mid_var: float32 [2, 2, 1632], replicated, may hold values from 0.05 to 20
- out_mean: float32 [2, 272], replicated, may hold values from -4 to 4
- out_var: float32 [2, 272], replicated, may hold values from 0.05 to 20
Outputs:
- block_output: bfloat16 [512, 12, 12, 272], P(('row', 'col'))
- mid_mean_new: float32 [2, 2, 1632], replicated
- mid_var_new: float32 [2, 2, 1632], replicated
- out_mean_new: float32 [2, 272], replicated
- out_var_new: float32 [2, 272], replicated
All inputs are finite; a program needn't handle non-finite values.
Results may differ from a plain program's by a relative error of at most 0.0049.
The roundings to bfloat16 on the way count: a program that leaves them out, or rounds other values in their place, can miss the bound.
Values sent between devices are 32-bit elements; how exact they have to be, the bound alone decides.
A program may use at most 128 MiB of HBM per device.

v0:
```python
import jax
import jax.numpy as jnp
from jax import lax
from jax.sharding import PartitionSpec as P

KERN = 5
LAYERS = 2


EPSILON = 0.001
RATIO_MAX = 3.0
SHIFT_MAX = 5.0
MOMENTUM = 0.01


def coefficients(first_sum, second_sum, row_count, run_mean, run_var, gain, bias):
    offset = first_sum / row_count
    batch_var = second_sum / row_count - offset * offset
    batch_mean = run_mean + offset
    batch_sigma = jnp.sqrt(batch_var + EPSILON)
    run_sigma = jnp.sqrt(run_var + EPSILON)
    scale_ratio = jnp.clip(batch_sigma / run_sigma, 1.0 / RATIO_MAX, RATIO_MAX)
    shift_clip = jnp.clip(offset / run_sigma, -SHIFT_MAX, SHIFT_MAX)
    gain_scale = gain * scale_ratio / batch_sigma
    gain_shift = bias + gain * shift_clip - batch_mean * gain_scale
    new_mean = run_mean + MOMENTUM * offset
    new_var = run_var + MOMENTUM * (batch_var - run_var)
    return (gain_scale, gain_shift, new_mean, new_var)


def renorm(values, run_mean, run_var, gain, bias):
    centered = values - run_mean
    first_sum = jnp.sum(centered, axis=(0, 1, 2))
    second_sum = jnp.sum(centered * centered, axis=(0, 1, 2))
    row_count = float(
        values.shape[0]
        * values.shape[1]
        * values.shape[2]
        * lax.axis_size("row")
        * lax.axis_size("col")
    )
    first_sum, second_sum = lax.psum((first_sum, second_sum), "row")
    first_sum, second_sum = lax.psum((first_sum, second_sum), "col")
    return coefficients(first_sum, second_sum, row_count, run_mean, run_var, gain, bias)


def project_rows(images, matrix):
    leading = images.shape[:3]
    flat_rows = images.reshape(-1, images.shape[3])
    product = jnp.dot(flat_rows, matrix, preferred_element_type=jnp.float32)
    return product.reshape(leading + (matrix.shape[1],))


def depthwise(active, kernel):
    reach = KERN // 2
    side_len = active.shape[1]
    padded = jnp.pad(active, ((0, 0), (reach, reach), (reach, reach), (0, 0)))
    running_total = jnp.zeros(active.shape, jnp.float32)
    for row_step in range(KERN):
        for col_step in range(KERN):
            window = padded[:, row_step : row_step + side_len, col_step : col_step + side_len, :]
            running_total = running_total + window * kernel[row_step * KERN + col_step]
    return running_total


def excite(lifted, reduce_w, reduce_b, grow_w, grow_b):
    pooled = jnp.mean(lifted, axis=(1, 2))
    squeezed = jax.nn.silu(jnp.dot(pooled, reduce_w, precision=lax.Precision.HIGHEST) + reduce_b)
    se_gate = jax.nn.sigmoid(jnp.dot(squeezed, grow_w, precision=lax.Precision.HIGHEST) + grow_b)
    return (lifted * se_gate[:, None, None, :]).astype(jnp.bfloat16)


def per_device(
    images,
    expand_weight,
    depth_kernel,
    squeeze_weight,
    squeeze_bias,
    excite_weight,
    excite_bias,
    project_weight,
    mid_gain,
    mid_bias,
    out_gain,
    out_bias,
    mid_mean,
    mid_var,
    out_mean,
    out_var,
):
    current = images
    mean_layers, var_layers, out_means, out_vars = ([], [], [], [])
    for layer_index in range(LAYERS):
        expanded = project_rows(current, expand_weight[layer_index])
        first_coef = renorm(
            expanded,
            mid_mean[layer_index, 0],
            mid_var[layer_index, 0],
            mid_gain[layer_index, 0],
            mid_bias[layer_index, 0],
        )
        active = jax.nn.silu(expanded * first_coef[0] + first_coef[1]).astype(jnp.bfloat16)
        spread = depthwise(active, depth_kernel[layer_index])
        second_coef = renorm(
            spread,
            mid_mean[layer_index, 1],
            mid_var[layer_index, 1],
            mid_gain[layer_index, 1],
            mid_bias[layer_index, 1],
        )
        lifted = jax.nn.silu(spread * second_coef[0] + second_coef[1])
        scaled = excite(
            lifted,
            squeeze_weight[layer_index],
            squeeze_bias[layer_index],
            excite_weight[layer_index],
            excite_bias[layer_index],
        )
        projected = project_rows(scaled, project_weight[layer_index])
        third_coef = renorm(
            projected,
            out_mean[layer_index],
            out_var[layer_index],
            out_gain[layer_index],
            out_bias[layer_index],
        )
        current = (current.astype(jnp.float32) + projected * third_coef[0] + third_coef[1]).astype(
            jnp.bfloat16
        )
        mean_layers.append(jnp.stack([first_coef[2], second_coef[2]]))
        var_layers.append(jnp.stack([first_coef[3], second_coef[3]]))
        out_means.append(third_coef[2])
        out_vars.append(third_coef[3])
    return (
        current,
        jnp.stack(mean_layers),
        jnp.stack(var_layers),
        jnp.stack(out_means),
        jnp.stack(out_vars),
    )


def solution(mesh):
    in_specs = (
        P(("row", "col"), None, None, None),
        P(),
        P(),
        P(),
        P(),
        P(),
        P(),
        P(),
        P(),
        P(),
        P(),
        P(),
        P(),
        P(),
        P(),
        P(),
    )
    out_specs = (P(("row", "col"), None, None, None), P(), P(), P(), P())
    return jax.shard_map(
        per_device, mesh=mesh, in_specs=in_specs, out_specs=out_specs, check_vma=False
    )
```

profile of v0, /device:TPU:0, one launch (start us, length us, event | category | flops | bytes accessed | tf_op | source)
XLA Modules:
  0.0 407.2 jit_solution(3430240509740645295)
XLA Ops:
  4.6 0.9 slice_reduce_fusion.33
  5.4 0.9 slice_reduce_fusion.32
  6.3 1.0 slice_reduce_fusion.2
  7.3 1.1 slice_reduce_fusion.6
  8.4 1.2 slice_reduce_fusion.28
  9.6 1.3 slice_reduce_fusion.29
  10.9 2.2 fusion.46
  13.1 2.3 fusion.47
  15.4 11.5 %multiply_reduce_fusion.3 = (f32[1632]{0:T(1024)S(1)}, f32[1632]{0:T(1024)S(1)}, f32[16,12,12,1632]{3,0,2,1:T(8,128)}) fusion(f32[1632]{0:T(1024)S(1)} %get-tuple-element.81, bf16[16,12,12,272]{3,0,2,1:T(8,128)(2,1)} %param.16, bf16[2,272,1632]{2,1,0:T(8,128)(2,1)} %param.17), kind=kOutput, calls=%fused_computation.59 | convolution fusion | flops 2060546816 | bytes 17734784 | tf_op jit(solution)/shard_map/dot_general | solution.py:50
  27.0 30.3 %all-reduce.7 = (f32[1632]{0:T(1024)S(1)}, f32[1632]{0:T(1024)S(1)}) all-reduce(f32[1632]{0:T(1024)S(1)} %get-tuple-element.12, f32[1632]{0:T(1024)S(1)} %get-tuple-element.11), channel_id=1, replica_groups=mesh['row'=8,'col'=4] {'row'}, use_global_device_ids=true, to_apply=%region_4.0 | all-reduce | flops 3264 | bytes 26112 | tf_op jit(solution)/shard_map/psum | solution.py:42
  57.3 16.0 %all-reduce.13 = (f32[1632]{0:T(1024)S(1)}, f32[1632]{0:T(1024)S(1)}) all-reduce(f32[1632]{0:T(1024)S(1)} %get-tuple-element.103, f32[1632]{0:T(1024)S(1)} %get-tuple-element.104), channel_id=1, replica_groups=mesh['row'=8,'col'=4] {'col'}, use_global_device_ids=true, to_apply=%region_5.0 | all-reduce | flops 3264 | bytes 26112 | tf_op jit(solution)/shard_map/psum | solution.py:43
  73.3 7.8 %multiply_convert_fusion.3 = bf16[16,12,12,1632]{3,0,2,1:T(8,128)(2,1)S(1)} fusion(f32[16,12,12,1632]{3,0,2,1:T(8,128)} %get-tuple-element.149, f32[1632]{0:T(1024)S(1)} %get-tuple-element.130, f32[1632]{0:T(1024)S(1)} %get-tuple-element.129), kind=kLoop, calls=%fused_computation.58 | loop fusion | flops 26320896 | bytes 22573824 | tf_op jit(solution)/shard_map/convert_element_type | solution.py:102
  81.2 50.2 %multiply_reduce_fusion.2 = (f32[1632]{0:T(1024)S(1)}, f32[1632]{0:T(1024)S(1)}, f32[16,12,12,1632]{3,0,2,1:T(8,128)}) fusion(f32[1632]{0:T(1024)S(1)} %get-tuple-element.80, f32[1632]{0:T(1024)S(1)} %get-tuple-element.40, f32[1632]{0:T(1024)S(1)} %get-tuple-element.41, f32[1632]{0:T(1024)S(1)} %get-tuple-element.42, f32[1632]{0:T(1024)S(1)} %get-tuple-element.43, ...), kind=kLoop, calls=%fused_computation.56 | loop fusion | flops 293286720 | bytes 22743552 | tf_op jit(solution)/shard_map/reduce_sum | solution.py:34
  131.4 26.1 %all-reduce.6 = (f32[1632]{0:T(1024)S(1)}, f32[1632]{0:T(1024)S(1)}) all-reduce(f32[1632]{0:T(1024)S(1)} %get-tuple-element.10, f32[1632]{0:T(1024)S(1)} %get-tuple-element.9), channel_id=1, replica_groups=mesh['row'=8,'col'=4] {'row'}, use_global_device_ids=true, to_apply=%region_10.11 | all-reduce | flops 3264 | bytes 26112 | tf_op jit(solution)/shard_map/psum | solution.py:42
  157.5 13.7 %all-reduce.12 = (f32[1632]{0:T(1024)S(1)}, f32[1632]{0:T(1024)S(1)}) all-reduce(f32[1632]{0:T(1024)S(1)} %get-tuple-element.101, f32[1632]{0:T(1024)S(1)} %get-tuple-element.102), channel_id=1, replica_groups=mesh['row'=8,'col'=4] {'col'}, use_global_device_ids=true, to_apply=%region_11.12 | all-reduce | flops 3264 | bytes 26112 | tf_op jit(solution)/shard_map/psum | solution.py:43
  171.3 8.0 %fusion.22 = f32[16,1632]{1,0:T(8,128)S(1)} fusion(f32[1632]{0:T(1024)S(1)} %get-tuple-element.128, f32[16,12,12,1632]{3,0,2,1:T(8,128)} %get-tuple-element.118, f32[1632]{0:T(1024)S(1)} %get-tuple-element.127), kind=kLoop, calls=%fused_computation.96 | loop fusion | flops 26294784 | bytes 15158016 | tf_op jit(solution)/shard_map/reduce_sum | solution.py:67
  181.0 7.5 %multiply_reduce_fusion.5 = (f32[272]{0:T(512)S(1)}, f32[272]{0:T(512)S(1)}, f32[16,12,12,272]{3,0,2,1:T(8,128)}) fusion(f32[272]{0:T(512)S(1)} %get-tuple-element.92, bf16[2,1632,272]{1,2,0:T(8,128)(2,1)} %param.23, f32[16,1632]{1,0:T(8,128)S(1)} %fusion.7, f32[1632]{0:T(1024)S(1)} %get-tuple-element.128, f32[16,12,12,1632]{3,0,2,1:T(8,128)S(1)} %copy-done.1, ...), kind=kOutput, calls=%fused_computation.71 | convolution fusion | flops 2078096896 | bytes 18573248 | tf_op jit(solution)/shard_map/dot_general | solution.py:50
  188.5 13.6 %all-reduce.5 = (f32[272]{0:T(512)S(1)}, f32[272]{0:T(512)S(1)}) all-reduce(f32[272]{0:T(512)S(1)} %get-tuple-element.16, f32[272]{0:T(512)S(1)} %get-tuple-element.15), channel_id=1, replica_groups=mesh['row'=8,'col'=4] {'row'}, use_global_device_ids=true, to_apply=%region_17.18 | all-reduce | flops 544 | bytes 4352 | tf_op jit(solution)/shard_map/psum | solution.py:42
  202.1 9.2 %all-reduce.11 = (f32[272]{0:T(512)S(1)}, f32[272]{0:T(512)S(1)}) all-reduce(f32[272]{0:T(512)S(1)} %get-tuple-element.99, f32[272]{0:T(512)S(1)} %get-tuple-element.100), channel_id=1, replica_groups=mesh['row'=8,'col'=4] {'col'}, use_global_device_ids=true, to_apply=%region_18.19 | all-reduce | flops 544 | bytes 4352 | tf_op jit(solution)/shard_map/psum | solution.py:43
  211.3 3.1 add_convert_fusion.1
  214.4 8.9 %multiply_reduce_fusion.1 = (f32[1632]{0:T(1024)S(1)}, f32[1632]{0:T(1024)S(1)}, f32[16,12,12,1632]{3,0,2,1:T(8,128)}) fusion(f32[1632]{0:T(1024)S(1)} %get-tuple-element.79, bf16[16,12,12,272]{3,0,2,1:T(8,128)(2,1)S(1)} %add_convert_fusion.1, bf16[2,272,1632]{2,1,0:T(8,128)(2,1)} %param.17), kind=kOutput, calls=%fused_computation.53 | convolution fusion | flops 2060546816 | bytes 17218688 | tf_op jit(solution)/shard_map/dot_general | solution.py:50
  223.3 25.9 %all-reduce.4 = (f32[1632]{0:T(1024)S(1)}, f32[1632]{0:T(1024)S(1)}) all-reduce(f32[1632]{0:T(1024)S(1)} %get-tuple-element.8, f32[1632]{0:T(1024)S(1)} %get-tuple-element.7), channel_id=1, replica_groups=mesh['row'=8,'col'=4] {'row'}, use_global_device_ids=true, to_apply=%region_23.24 | all-reduce | flops 3264 | bytes 26112 | tf_op jit(solution)/shard_map/psum | solution.py:42
  249.2 14.1 %all-reduce.10 = (f32[1632]{0:T(1024)S(1)}, f32[1632]{0:T(1024)S(1)}) all-reduce(f32[1632]{0:T(1024)S(1)} %get-tuple-element.97, f32[1632]{0:T(1024)S(1)} %get-tuple-element.98), channel_id=1, replica_groups=mesh['row'=8,'col'=4] {'col'}, use_global_device_ids=true, to_apply=%region_24.25 | all-reduce | flops 3264 | bytes 26112 | tf_op jit(solution)/shard_map/psum | solution.py:43
  263.3 7.8 %multiply_convert_fusion.1 = bf16[16,12,12,1632]{3,0,2,1:T(8,128)(2,1)S(1)} fusion(f32[16,12,12,1632]{3,0,2,1:T(8,128)} %get-tuple-element.151, f32[1632]{0:T(1024)S(1)} %get-tuple-element.126, f32[1632]{0:T(1024)S(1)} %get-tuple-element.125), kind=kLoop, calls=%fused_computation.52 | loop fusion | flops 26320896 | bytes 22573824 | tf_op jit(solution)/shard_map/convert_element_type | solution.py:102
  271.2 50.2 %multiply_reduce_fusion = (f32[1632]{0:T(1024)S(1)}, f32[1632]{0:T(1024)S(1)}, f32[16,12,12,1632]{3,0,2,1:T(8,128)}) fusion(f32[1632]{0:T(1024)S(1)} %get-tuple-element.82, f32[1632]{0:T(1024)S(1)} %get-tuple-element.66, f32[1632]{0:T(1024)S(1)} %get-tuple-element.55, f32[1632]{0:T(1024)S(1)} %get-tuple-element.18, f32[1632]{0:T(1024)S(1)} %get-tuple-element.19, ...), kind=kLoop, calls=%fused_computation.50 | loop fusion | flops 293286720 | bytes 22743552 | tf_op jit(solution)/shard_map/reduce_sum | solution.py:34
  321.4 26.1 %all-reduce.3 = (f32[1632]{0:T(1024)S(1)}, f32[1632]{0:T(1024)S(1)}) all-reduce(f32[1632]{0:T(1024)S(1)} %get-tuple-element.6, f32[1632]{0:T(1024)S(1)} %get-tuple-element.5), channel_id=1, replica_groups=mesh['row'=8,'col'=4] {'row'}, use_global_device_ids=true, to_apply=%region_29.30 | all-reduce | flops 3264 | bytes 26112 | tf_op jit(solution)/shard_map/psum | solution.py:42
  347.5 15.0 %all-reduce.9 = (f32[1632]{0:T(1024)S(1)}, f32[1632]{0:T(1024)S(1)}) all-reduce(f32[1632]{0:T(1024)S(1)} %get-tuple-element.95, f32[1632]{0:T(1024)S(1)} %get-tuple-element.96), channel_id=1, replica_groups=mesh['row'=8,'col'=4] {'col'}, use_global_device_ids=true, to_apply=%region_30.31 | all-reduce | flops 3264 | bytes 26112 | tf_op jit(solution)/shard_map/psum | solution.py:43
  363.9 8.4 %fusion.23 = f32[16,1632]{1,0:T(8,128)S(1)} fusion(f32[1632]{0:T(1024)S(1)} %get-tuple-element.124, f32[16,12,12,1632]{3,0,2,1:T(8,128)} %get-tuple-element.117, f32[1632]{0:T(1024)S(1)} %get-tuple-element.123), kind=kLoop, calls=%fused_computation.97 | loop fusion | flops 26294784 | bytes 15158016 | tf_op jit(solution)/shard_map/reduce_sum | solution.py:67
  373.3 7.5 %multiply_reduce_fusion.4 = (f32[272]{0:T(512)S(1)}, f32[272]{0:T(512)S(1)}, f32[16,12,12,272]{3,0,2,1:T(8,128)}) fusion(f32[272]{0:T(512)S(1)} %get-tuple-element.91, bf16[2,1632,272]{1,2,0:T(8,128)(2,1)} %param.23, f32[16,1632]{1,0:T(8,128)S(1)} %fusion.11, f32[1632]{0:T(1024)S(1)} %get-tuple-element.124, f32[16,12,12,1632]{3,0,2,1:T(8,128)S(1)} %copy-done, ...), kind=kOutput, calls=%fused_computation.69 | convolution fusion | flops 2078096896 | bytes 18573248 | tf_op jit(solution)/shard_map/dot_general | solution.py:50
  380.7 13.6 %all-reduce.2 = (f32[272]{0:T(512)S(1)}, f32[272]{0:T(512)S(1)}) all-reduce(f32[272]{0:T(512)S(1)} %get-tuple-element.14, f32[272]{0:T(512)S(1)} %get-tuple-element.13), channel_id=1, replica_groups=mesh['row'=8,'col'=4] {'row'}, use_global_device_ids=true, to_apply=%region_36.37 | all-reduce | flops 544 | bytes 4352 | tf_op jit(solution)/shard_map/psum | solution.py:42
  394.3 7.9 %all-reduce.8 = (f32[272]{0:T(512)S(1)}, f32[272]{0:T(512)S(1)}) all-reduce(f32[272]{0:T(512)S(1)} %get-tuple-element.93, f32[272]{0:T(512)S(1)} %get-tuple-element.94), channel_id=1, replica_groups=mesh['row'=8,'col'=4] {'col'}, use_global_device_ids=true, to_apply=%region_37.38 | all-reduce | flops 544 | bytes 4352 | tf_op jit(solution)/shard_map/psum | solution.py:43
  402.3 3.8 add_convert_fusion
  (39 shorter events, 9.3 us)
Async XLA Ops:
  171.2 9.8 %copy-start.1 = (f32[16,12,12,1632]{3,0,2,1:T(8,128)S(1)}, f32[16,12,12,1632]{3,0,2,1:T(8,128)}, u32[]{:S(2)}) copy-start(f32[16,12,12,1632]{3,0,2,1:T(8,128)} %get-tuple-element.118) | copy-start | bytes 45121540
  362.5 10.7 %copy-start = (f32[16,12,12,1632]{3,0,2,1:T(8,128)S(1)}, f32[16,12,12,1632]{3,0,2,1:T(8,128)}, u32[]{:S(2)}) copy-start(f32[16,12,12,1632]{3,0,2,1:T(8,128)} %get-tuple-element.117) | copy-start | bytes 45121540
where the time goes:
time: 409 us; the launch traced here: 407 us
  blocking collectives  212 us (52%)
  other arithmetic  142 us (35%)
  matrix products  37.1 us (9%)
  local copies, waits for them, and re-layouts  15.6 us (4%)
    psum x6, blocking collectives, renorm(): first_sum, second_sum = lax.psum((first_sum, second_sum), 'row')  136 us
    reduce_sum x2, other arithmetic, renorm(): second_sum = jnp.sum(centered * centered, axis=(0, 1, 2))  100 us
    psum x6, blocking collectives, renorm(): first_sum, second_sum = lax.psum((first_sum, second_sum), 'col')  76.1 us
    dot_general x4, matrix products, project_rows(): product = jnp.dot(flat_rows, matrix, preferred_element_type=jnp.float32)  35.3 us
    reduce_sum x2, other arithmetic, excite(): pooled = jnp.mean(lifted, axis=(1, 2))  16.4 us
    convert_element_type x2, other arithmetic, per_device(): jax.nn.silu(expanded * first_coef[0] + first_coef[1]).astype(jnp.bfloat16)  15.6 us

commit v1 on v0

v1 whole, which is shorter than its diff:
```python
import functools

import jax
import jax.numpy as jnp
from jax import lax
from jax.experimental import pallas as pl
from jax.experimental.pallas import tpu as pltpu
from jax.sharding import PartitionSpec as P

KERN = 5
REACH = KERN // 2
LANES = 128
WIDE = 2 * LANES

EPSILON = 0.001
RATIO_MAX = 3.0
SHIFT_MAX = 5.0
MOMENTUM = 0.01

VMEM_BYTES = 60 * 1024 * 1024


def coefficients(first_sum, second_sum, row_count, run_mean, run_var, gain, bias):
    offset = first_sum / row_count
    batch_var = second_sum / row_count - offset * offset
    batch_mean = run_mean + offset
    batch_sigma = jnp.sqrt(batch_var + EPSILON)
    run_sigma = jnp.sqrt(run_var + EPSILON)
    scale_ratio = jnp.clip(batch_sigma / run_sigma, 1.0 / RATIO_MAX, RATIO_MAX)
    shift_clip = jnp.clip(offset / run_sigma, -SHIFT_MAX, SHIFT_MAX)
    gain_scale = gain * scale_ratio / batch_sigma
    gain_shift = bias + gain * shift_clip - batch_mean * gain_scale
    new_mean = run_mean + MOMENTUM * offset
    new_var = run_var + MOMENTUM * (batch_var - run_var)
    return (gain_scale, gain_shift, new_mean, new_var)


def half_silu(half_value):
    return half_value + half_value * jnp.tanh(half_value)


def fold_rows(values):
    return jnp.sum(values.reshape(-1, 8, values.shape[-1]), axis=0)


def exchange_kernel(n_row, n_col, x_ref, o_ref, buf_row, part, buf_col, s_row, r_row, s_col, r_col):
    row = lax.axis_index("row")
    col = lax.axis_index("col")
    row_peers = [lax.rem(row + k, n_row) for k in range(1, n_row)]
    col_peers = [lax.rem(col + k, n_col) for k in range(1, n_col)]
    mesh_id = pl.DeviceIdType.MESH
    barrier = pltpu.get_barrier_semaphore()
    for peer in row_peers:
        pl.semaphore_signal(barrier, inc=1, device_id=(peer, col), device_id_type=mesh_id)
    for peer in col_peers:
        pl.semaphore_signal(barrier, inc=1, device_id=(row, peer), device_id_type=mesh_id)
    pl.semaphore_wait(barrier, len(row_peers) + len(col_peers))

    copies = []
    for k, peer in enumerate(row_peers):
        copy = pltpu.make_async_remote_copy(
            src_ref=x_ref,
            dst_ref=buf_row.at[row],
            send_sem=s_row.at[k],
            recv_sem=r_row.at[k],
            device_id=(peer, col),
            device_id_type=mesh_id,
        )
        copy.start()
        copies.append(copy)
    buf_row[row] = x_ref[...]
    for copy in copies:
        copy.wait()
    total = buf_row[0]
    for k in range(1, n_row):
        total = total + buf_row[k]
    part[...] = total
    copies = []
    for k, peer in enumerate(col_peers):
        copy = pltpu.make_async_remote_copy(
            src_ref=part,
            dst_ref=buf_col.at[col],
            send_sem=s_col.at[k],
            recv_sem=r_col.at[k],
            device_id=(row, peer),
            device_id_type=mesh_id,
        )
        copy.start()
        copies.append(copy)
    buf_col[col] = total
    for copy in copies:
        copy.wait()
    total = buf_col[0]
    for k in range(1, n_col):
        total = total + buf_col[k]
    o_ref[...] = total


def all_sum(stats, n_row, n_col, collective_id):
    shape = stats.shape
    vmem = pl.BlockSpec(memory_space=pltpu.VMEM)
    return pl.pallas_call(
        functools.partial(exchange_kernel, n_row, n_col),
        out_shape=jax.ShapeDtypeStruct(shape, jnp.float32),
        in_specs=[vmem],
        out_specs=vmem,
        scratch_shapes=[
            pltpu.VMEM((n_row,) + shape, jnp.float32),
            pltpu.VMEM(shape, jnp.float32),
            pltpu.VMEM((n_col,) + shape, jnp.float32),
            pltpu.SemaphoreType.DMA((n_row - 1,)),
            pltpu.SemaphoreType.DMA((n_row - 1,)),
            pltpu.SemaphoreType.DMA((n_col - 1,)),
            pltpu.SemaphoreType.DMA((n_col - 1,)),
        ],
        compiler_params=pltpu.CompilerParams(collective_id=collective_id, has_side_effects=True),
    )(stats)


def expand_stats_kernel(chunk, x_ref, w_ref, mean_ref, stats_ref):
    mean = mean_ref[0, 0:1, :]
    weight = w_ref[0]

    def body(step, carry):
        rows = pl.ds(pl.multiple_of(step * chunk, chunk), chunk)
        y = jnp.dot(x_ref[rows, :], weight, preferred_element_type=jnp.float32)
        centered = y - mean
        return carry[0] + fold_rows(centered), carry[1] + fold_rows(centered * centered)

    zero = jnp.zeros((8, weight.shape[1]), jnp.float32)
    first, second = lax.fori_loop(0, x_ref.shape[0] // chunk, body, (zero, zero))
    stats_ref[0:1, :] = jnp.sum(first, axis=0, keepdims=True)
    stats_ref[1:2, :] = jnp.sum(second, axis=0, keepdims=True)


def residual_kernel(
    layer, chunk, row_count, x_ref, p_ref, s_ref, m_ref, v_ref, g_ref, b_ref, w_ref, mean_ref,
    cur_ref, stats_ref, nm_ref, nv_ref,
):
    @pl.when(pl.program_id(0) == 0)
    def _():
        pick = slice(layer, layer + 1)
        scale, shift, new_mean, new_var = coefficients(
            s_ref[0:1, :], s_ref[1:2, :], row_count,
            m_ref[pick, :], v_ref[pick, :], g_ref[pick, :], b_ref[pick, :],
        )
        nm_ref[...] = new_mean
        nv_ref[...] = new_var

        def body(step, carry):
            rows = pl.ds(pl.multiple_of(step * chunk, chunk), chunk)
            cur_ref[rows, :] = (
                x_ref[rows, :].astype(jnp.float32) + p_ref[rows, :] * scale + shift
            ).astype(jnp.bfloat16)
            return carry

        lax.fori_loop(0, x_ref.shape[0] // chunk, body, 0)

    expand_stats_kernel(chunk, cur_ref, w_ref, mean_ref, stats_ref)


def spread_kernel(
    side, batch, row_count, blocks, x_ref, w_ref, dk_ref, sums_ref, mean_ref, var_ref, gain_ref, bias_ref,
    spread_ref, stats_ref, nm_ref, nv_ref, act, taps,
):
    chunk = side * batch
    scale, shift, new_mean, new_var = coefficients(
        sums_ref[0:1, :], sums_ref[1:2, :], row_count,
        mean_ref[0, 0:1, :], var_ref[0, 0:1, :], gain_ref[0, 0:1, :], bias_ref[0, 0:1, :],
    )
    nm_ref[...] = new_mean
    nv_ref[...] = new_var
    half_scale, half_shift = 0.5 * scale, 0.5 * shift
    weight = w_ref[0]

    def activate(step, carry):
        rows = pl.ds(pl.multiple_of(step * chunk, chunk), chunk)
        y = jnp.dot(x_ref[rows, :], weight, preferred_element_type=jnp.float32)
        active = half_silu(y * half_scale + half_shift).astype(jnp.bfloat16).astype(jnp.float32)
        for half in range(2):
            act[half, step] = active[:, half * LANES : (half + 1) * LANES].reshape(side, batch, LANES)
        return carry

    lax.fori_loop(0, side, activate, 0)

    def half_block(half, carry):
        lanes = pl.ds(pl.multiple_of(half * LANES, LANES), LANES)
        for tap in range(KERN * KERN):
            taps[tap] = jnp.broadcast_to(dk_ref[0, tap : tap + 1, lanes], (8, LANES))
        mean = jnp.broadcast_to(mean_ref[0, 1:2, lanes], (8, LANES))

        def row(h, steps, sums):
            first, second = sums
            for sub in range(batch // 8):
                total = [None] * side
                for dy in steps:
                    line = [act[half, h + dy - REACH, w, sub * 8 : sub * 8 + 8, :] for w in range(side)]
                    for dx in range(KERN):
                        tap = taps[dy * KERN + dx]
                        for w in range(side):
                            source = w + dx - REACH
                            if 0 <= source < side:
                                term = line[source] * tap
                                total[w] = term if total[w] is None else total[w] + term
                for w in range(side):
                    start = pl.multiple_of((h * side + w) * batch + sub * 8, 8)
                    spread_ref[half, pl.ds(start, 8), :] = total[w]
                    centered = total[w] - mean
                    first = first + centered
                    second = second + centered * centered
            return first, second

        zero = jnp.zeros((8, LANES), jnp.float32)
        sums = (zero, zero)
        for h in range(REACH):
            sums = row(h, range(REACH - h, KERN), sums)
        sums = lax.fori_loop(REACH, side - REACH, lambda h, c: row(h, range(KERN), c), sums)
        for h in range(side - REACH, side):
            sums = row(h, range(0, side - h + REACH), sums)
        stats_ref[0:1, lanes] = jnp.sum(sums[0], axis=0, keepdims=True)
        stats_ref[1:2, lanes] = jnp.sum(sums[1], axis=0, keepdims=True)
        return carry

    halves = jnp.minimum(2, blocks - 2 * pl.program_id(0))
    lax.fori_loop(0, halves, half_block, 0)


def lift_kernel(
    layer, side, batch, row_count, mid, v_ref, sums_ref, mean_ref, var_ref, gain_ref, bias_ref,
    sw_ref, sb_ref, ew_ref, eb_ref, pw_ref, om_ref, proj_ref, stats_ref, nm_ref, nv_ref,
    lifted, pooled, gate, scaled,
):
    chunk = side * batch
    block = pl.program_id(0)
    blocks = pl.num_programs(0)
    scale, shift, new_mean, new_var = coefficients(
        sums_ref[0:1, :], sums_ref[1:2, :], row_count,
        mean_ref[0, 1:2, :], var_ref[0, 1:2, :], gain_ref[0, 1:2, :], bias_ref[0, 1:2, :],
    )
    nm_ref[...] = new_mean
    nv_ref[...] = new_var
    half_scale, half_shift = 0.5 * scale, 0.5 * shift

    def lift(step, total):
        rows = pl.ds(pl.multiple_of(step * chunk, chunk), chunk)
        value = half_silu(v_ref[0, rows, :] * half_scale + half_shift)
        lifted[block, rows, :] = value
        return total + jnp.sum(value.reshape(side, batch, LANES), axis=0)

    total = lax.fori_loop(0, side, lift, jnp.zeros((batch, LANES), jnp.float32))
    pooled[:, pl.ds(pl.multiple_of(block * LANES, LANES), LANES)] = total / float(side * side)

    @pl.when(block == blocks - 1)
    def _():
        pick = slice(layer, layer + 1)
        squeezed = jnp.dot(
            pooled[:, :mid], sw_ref[0], precision=lax.Precision.HIGHEST, preferred_element_type=jnp.float32
        )
        squeezed = half_silu(0.5 * (squeezed + sb_ref[pick, :]))
        grown = jnp.dot(
            squeezed, ew_ref[0], precision=lax.Precision.HIGHEST, preferred_element_type=jnp.float32
        )
        gate[:, :mid] = 0.5 + 0.5 * jnp.tanh(0.5 * (grown + eb_ref[pick, :]))
        out_mean = om_ref[pick, :]

        def project(step, sums):
            rows = pl.ds(pl.multiple_of(step * chunk, chunk), chunk)
            for index in range(pl.cdiv(mid, LANES)):
                start = index * LANES
                stop = min(mid, start + LANES)
                value = lifted[index, rows, :].reshape(side, batch, LANES) * gate[:, start : start + LANES]
                value = value.astype(jnp.bfloat16).reshape(chunk, LANES)
                scaled[:, start:stop] = value[:, : stop - start]
            product = jnp.dot(scaled[...], pw_ref[0], preferred_element_type=jnp.float32)
            proj_ref[rows, :] = product
            centered = product - out_mean
            return sums[0] + fold_rows(centered), sums[1] + fold_rows(centered * centered)

        zero = jnp.zeros((8, proj_ref.shape[1]), jnp.float32)
        first, second = lax.fori_loop(0, side, project, (zero, zero))
        stats_ref[0:1, :] = jnp.sum(first, axis=0, keepdims=True)
        stats_ref[1:2, :] = jnp.sum(second, axis=0, keepdims=True)


def whole(shape):
    return pl.BlockSpec(shape, lambda j: (0,) * len(shape))


def of_layer(shape, layer):
    return pl.BlockSpec((1,) + shape[1:], lambda j: (layer,) + (0,) * (len(shape) - 1))


def columns(rows, width):
    return pl.BlockSpec((rows, width), lambda j: (0, j))


def layer_columns(rows, width, layer):
    return pl.BlockSpec((1, rows, width), lambda j: (layer, 0, j))


def f32(*shape):
    return jax.ShapeDtypeStruct(shape, jnp.float32)


PARAMS = pltpu.CompilerParams(vmem_limit_bytes=VMEM_BYTES, dimension_semantics=("arbitrary",))


def per_device(n_row, n_col, *args):
    (
        images, expand_weight, depth_kernel, squeeze_weight, squeeze_bias, excite_weight, excite_bias,
        project_weight, mid_gain, mid_bias, out_gain, out_bias, mid_mean, mid_var, out_mean, out_var,
    ) = args
    batch, side, _, out = images.shape
    layers, _, mid = expand_weight.shape
    squeeze = squeeze_weight.shape[2]
    rows = side * side * batch
    chunk = side * batch
    row_count = float(rows * n_row * n_col)
    wide_steps = pl.cdiv(mid, WIDE)
    blocks = pl.cdiv(mid, LANES)
    taps_count = depth_kernel.shape[1]

    current = images.reshape(batch, side * side, out).transpose(1, 0, 2).reshape(rows, out)
    projected = None
    out_sums = None
    means, variances, out_means, out_vars = [], [], [], []
    for layer in range(layers):
        wide_params = [layer_columns(2, WIDE, layer)] * 4
        weight_spec = layer_columns(out, WIDE, layer)
        if layer == 0:
            stats = pl.pallas_call(
                functools.partial(expand_stats_kernel, chunk),
                grid=(wide_steps,),
                in_specs=[whole((rows, out)), weight_spec, wide_params[0]],
                out_specs=columns(2, WIDE),
                out_shape=f32(2, mid),
                compiler_params=PARAMS,
            )(current, expand_weight, mid_mean)
        else:
            current, stats, new_mean, new_var = pl.pallas_call(
                functools.partial(residual_kernel, layer - 1, chunk, row_count),
                grid=(wide_steps,),
                in_specs=[whole((rows, out)), whole((rows, out)), whole((2, out))]
                + [whole((layers, out))] * 4
                + [weight_spec, wide_params[0]],
                out_specs=[whole((rows, out)), columns(2, WIDE), whole((1, out)), whole((1, out))],
                out_shape=[jax.ShapeDtypeStruct((rows, out), jnp.bfloat16), f32(2, mid), f32(1, out), f32(1, out)],
                compiler_params=PARAMS,
            )(current, projected, out_sums, out_mean, out_var, out_gain, out_bias, expand_weight, mid_mean)
            out_means.append(new_mean)
            out_vars.append(new_var)
        sums = all_sum(stats, n_row, n_col, 1)
        spread, stats, mean_a, var_a = pl.pallas_call(
            functools.partial(spread_kernel, side, batch, row_count, blocks),
            grid=(wide_steps,),
            in_specs=[whole((rows, out)), weight_spec, layer_columns(taps_count, WIDE, layer), columns(2, WIDE)]
            + wide_params,
            out_specs=[
                pl.BlockSpec((2, rows, LANES), lambda j: (j, 0, 0)),
                columns(2, WIDE), columns(1, WIDE), columns(1, WIDE),
            ],
            out_shape=[f32(2 * wide_steps, rows, LANES), f32(2, mid), f32(1, mid), f32(1, mid)],
            scratch_shapes=[
                pltpu.VMEM((2, side, side, batch, LANES), jnp.float32),
                pltpu.VMEM((taps_count, 8, LANES), jnp.float32),
            ],
            compiler_params=PARAMS,
        )(current, expand_weight, depth_kernel, sums, mid_mean, mid_var, mid_gain, mid_bias)
        sums = all_sum(stats, n_row, n_col, 1)
        projected, stats, mean_b, var_b = pl.pallas_call(
            functools.partial(lift_kernel, layer, side, batch, row_count, mid),
            grid=(blocks,),
            in_specs=[pl.BlockSpec((1, rows, LANES), lambda j: (j, 0, 0)), columns(2, LANES)]
            + [layer_columns(2, LANES, layer)] * 4
            + [
                of_layer(squeeze_weight.shape, layer), whole(squeeze_bias.shape),
                of_layer(excite_weight.shape, layer), whole(excite_bias.shape),
                of_layer(project_weight.shape, layer), whole(out_mean.shape),
            ],
            out_specs=[whole((rows, out)), whole((2, out)), columns(1, LANES), columns(1, LANES)],
            out_shape=[f32(rows, out), f32(2, out), f32(1, mid), f32(1, mid)],
            scratch_shapes=[
                pltpu.VMEM((blocks, rows, LANES), jnp.float32),
                pltpu.VMEM((batch, blocks * LANES), jnp.float32),
                pltpu.VMEM((batch, blocks * LANES), jnp.float32),
                pltpu.VMEM((chunk, mid), jnp.bfloat16),
            ],
            compiler_params=PARAMS,
        )(
            spread, sums, mid_mean, mid_var, mid_gain, mid_bias,
            squeeze_weight, squeeze_bias, excite_weight, excite_bias, project_weight, out_mean,
        )
        out_sums = all_sum(stats, n_row, n_col, 2)
        means += [mean_a, mean_b]
        variances += [var_a, var_b]
    last = layers - 1
    scale, shift, new_mean, new_var = coefficients(
        out_sums[0], out_sums[1], row_count, out_mean[last], out_var[last], out_gain[last], out_bias[last]
    )
    out_means.append(new_mean[None])
    out_vars.append(new_var[None])
    current = (current.astype(jnp.float32) + projected * scale + shift).astype(jnp.bfloat16)
    current = current.reshape(side * side, batch, out).transpose(1, 0, 2).reshape(images.shape)
    return (
        current,
        jnp.concatenate(means).reshape(mid_mean.shape),
        jnp.concatenate(variances).reshape(mid_var.shape),
        jnp.concatenate(out_means),
        jnp.concatenate(out_vars),
    )


def solution(mesh):
    images_spec = P(("row", "col"), None, None, None)
    return jax.shard_map(
        functools.partial(per_device, mesh.shape["row"], mesh.shape["col"]),
        mesh=mesh,
        in_specs=(images_spec,) + (P(),) * 15,
        out_specs=(images_spec, P(), P(), P(), P()),
        check_vma=False,
    )
```

time: 409 us -> 262 us (0.64)
  Pallas kernels: 0 us -> 246 us
  blocking collectives: 212 us -> 0 us
  other arithmetic: 142 us -> 5.94 us
  matrix products: 37.1 us -> 0 us
  local copies, waits for them, and re-layouts: 15.6 us -> 8.54 us
    pallas_call x0 -> x12, Pallas kernels: none -> 246 us  [the longest x2 90.9 us: per_device(): pl.pallas_call(functools.partial(spread_kernel, side, batch, row_count, b...]
    psum x12 -> x0, blocking collectives: 212 us -> none  [the longest x6 136 us: renorm(): first_sum, second_sum = lax.psum((first_sum, second_sum), 'row')]
    reduce_sum x4 -> x0, other arithmetic: 117 us -> none  [the longest x2 100 us: renorm(): second_sum = jnp.sum(centered * centered, axis=(0, 1, 2))]
    dot_general x8 -> x0, matrix products: 37.1 us -> none  [the longest x4 35.3 us: project_rows(): product = jnp.dot(flat_rows, matrix, preferred_element_type=jnp.float32)]
    convert_element_type x4 -> x1, other arithmetic: 22.5 us -> 3.79 us  [per_device(): (current.astype(jnp.float32) + projected * scale + shift).astype(jnp.bflo...]
    slice x12 -> x0, local copies, waits for them, and re-layouts: 14 us -> none  [the longest x3 3.6 us: depthwise(): running_total = running_total + window * kernel[row_step * KERN + col_step]]
    unnamed x4 -> x40, local copies, waits for them, and re-layouts: 0.81 us -> 7.27 us
where the time goes in v1:
time: 262 us
  Pallas kernels  246 us (94%)
  local copies, waits for them, and re-layouts  8.54 us (3%)
  other arithmetic  5.94 us (2%)
    pallas_call x2, Pallas kernels, per_device(): pl.pallas_call(functools.partial(spread_kernel, side, batch, row_count, b...  90.9 us
    pallas_call x6, Pallas kernels, all_sum(): pl.pallas_call(functools.partial(exchange_kernel, n_row, n_col), out_shap...  68.1 us
    pallas_call x2, Pallas kernels, per_device(): pl.pallas_call(functools.partial(lift_kernel, layer, side, batch, row_cou...  44 us
    pallas_call x1, Pallas kernels, per_device(): pl.pallas_call(functools.partial(residual_kernel, layer - 1, chunk, row_c...  22.8 us
    pallas_call x1, Pallas kernels, per_device(): pl.pallas_call(functools.partial(expand_stats_kernel, chunk), grid=(wide_...  20.4 us
    unnamed x40, local copies, waits for them, and re-layouts  7.27 us

profile of v1, /device:TPU:0, one launch (start us, length us, event | category | flops | bytes accessed | tf_op | source)
XLA Modules:
  0.0 261.5 jit_solution(5639162882824849400)
XLA Ops:
  0.7 20.4 %shard_map.191.x_ref = f32[2,1632]{1,0:T(2,128)} custom-call(bf16[2304,272]{1,0:T(8,128)(2,1)} %bitcast.10, bf16[2,272,1632]{2,1,0:T(8,128)(2,1)} %w_ref.7, f32[2,2,1632]{2,1,0:T(2,128)} %mean_ref.11), custom_call_target="tpu_custom_call" | custom-call | tf_op jit(solution)/shard_map/pallas_call | solution.py:331
  21.1 13.7 %shard_map.192.sums_ref = f32[2,1632]{1,0:T(2,128)} custom-call(f32[2,1632]{1,0:T(2,128)} %shard_map.191.x_ref), custom_call_target="tpu_custom_call" | custom-call | tf_op jit(solution)/shard_map/pallas_call | solution.py:102
  34.7 0.0 copy-done.3
  34.7 0.8 copy.21.dk_ref
  35.6 1.1 copy.23.ew_ref
  36.7 2.6 copy.22.sw_ref
  39.2 2.7 %copy.24.pw_ref = bf16[2,1632,272]{2,1,0:T(8,128)(2,1)} copy(bf16[2,1632,272]{1,2,0:T(8,128)(2,1)S(1)} %copy-done.1) | data formatting | bytes 3551232 | tf_op args[7]
  41.9 45.4 %shard_map.193 = (f32[14,2304,128]{2,1,0:T(8,128)}, f32[2,1632]{1,0:T(2,128)}, f32[1,1632]{1,0:T(1,128)}, f32[1,1632]{1,0:T(1,128)}) custom-call(bf16[2304,272]{1,0:T(8,128)(2,1)} %bitcast.11, bf16[2,272,1632]{2,1,0:T(8,128)(2,1)} %w_ref.7, f32[2,25,1632]{2,1,0:T(8,128)} %copy.21.dk_ref, f32[2,1632]{1,0:T(2,128)} %shard_map.192.sums_ref, ...), custom_call_target="tpu_custom_call" | custom-call | tf_op jit(solution)/shard_map/pallas_call | solution.py:353
  87.4 11.2 %shard_map.194.sums_ref = f32[2,1632]{1,0:T(2,128)} custom-call(f32[2,1632]{1,0:T(2,128)} %get-tuple-element.26.x_ref), custom_call_target="tpu_custom_call" | custom-call | tf_op jit(solution)/shard_map/pallas_call | solution.py:102
  98.6 21.9 %shard_map.195 = (f32[2304,272]{1,0:T(8,128)}, f32[2,272]{1,0:T(2,128)}, f32[1,1632]{1,0:T(1,128)}, f32[1,1632]{1,0:T(1,128)}) custom-call(f32[14,2304,128]{2,1,0:T(8,128)} %get-tuple-element.25.v_ref, f32[2,1632]{1,0:T(2,128)} %shard_map.194.sums_ref, f32[2,2,1632]{2,1,0:T(2,128)} %mean_ref.11, f32[2,2,1632]{2,1,0:T(2,128)} %var_ref.7, ...), custom_call_target="tpu_custom_call" | custom-call | tf_op jit(solution)/shard_map/pallas_call | solution.py:370
  120.6 10.2 %shard_map.196.s_ref = f32[2,272]{1,0:T(2,128)} custom-call(f32[2,272]{1,0:T(2,128)} %get-tuple-element.28.x_ref), custom_call_target="tpu_custom_call" | custom-call | tf_op jit(solution)/shard_map/pallas_call | solution.py:102
  130.7 22.8 %shard_map.197 = (bf16[2304,272]{1,0:T(8,128)(2,1)}, f32[2,1632]{1,0:T(2,128)}, f32[1,272]{1,0:T(1,128)}, f32[1,272]{1,0:T(1,128)}) custom-call(bf16[2304,272]{1,0:T(8,128)(2,1)} %bitcast.12, f32[2304,272]{1,0:T(8,128)} %get-tuple-element.27.p_ref, f32[2,272]{1,0:T(2,128)} %shard_map.196.s_ref, f32[2,272]{1,0:T(2,128)} %om_ref.3, f32[2,272]{1,0:T(2,128)} %v_ref.1, ...), custom_call_target="tpu_custom_call" | custom-call | tf_op jit(solution)/shard_map/pallas_call | solution.py:340
  153.5 11.2 %shard_map.198.sums_ref = f32[2,1632]{1,0:T(2,128)} custom-call(f32[2,1632]{1,0:T(2,128)} %get-tuple-element.30.x_ref), custom_call_target="tpu_custom_call" | custom-call | tf_op jit(solution)/shard_map/pallas_call | solution.py:102
  164.7 45.5 %shard_map.199 = (f32[14,2304,128]{2,1,0:T(8,128)}, f32[2,1632]{1,0:T(2,128)}, f32[1,1632]{1,0:T(1,128)}, f32[1,1632]{1,0:T(1,128)}) custom-call(bf16[2304,272]{1,0:T(8,128)(2,1)} %get-tuple-element.29.x_ref, bf16[2,272,1632]{2,1,0:T(8,128)(2,1)} %w_ref.7, f32[2,25,1632]{2,1,0:T(8,128)} %copy.21.dk_ref, f32[2,1632]{1,0:T(2,128)} %shard_map.198.sums_ref, ...), custom_call_target="tpu_custom_call" | custom-call | tf_op jit(solution)/shard_map/pallas_call | solution.py:353
  210.2 10.9 %shard_map.200.sums_ref = f32[2,1632]{1,0:T(2,128)} custom-call(f32[2,1632]{1,0:T(2,128)} %get-tuple-element.32.x_ref), custom_call_target="tpu_custom_call" | custom-call | tf_op jit(solution)/shard_map/pallas_call | solution.py:102
  221.1 0.0 copy-start.5
  221.1 0.0 copy-start.4
  221.1 0.0 copy-start.6
  221.2 0.0 copy-start.7
  221.2 0.0 copy-start
  221.2 22.0 %shard_map.201 = (f32[2304,272]{1,0:T(8,128)}, f32[2,272]{1,0:T(2,128)}, f32[1,1632]{1,0:T(1,128)}, f32[1,1632]{1,0:T(1,128)}) custom-call(f32[14,2304,128]{2,1,0:T(8,128)} %get-tuple-element.31.v_ref, f32[2,1632]{1,0:T(2,128)} %shard_map.200.sums_ref, f32[2,2,1632]{2,1,0:T(2,128)} %mean_ref.11, f32[2,2,1632]{2,1,0:T(2,128)} %var_ref.7, ...), custom_call_target="tpu_custom_call" | custom-call | tf_op jit(solution)/shard_map/pallas_call | solution.py:370
  243.2 10.9 %shard_map.202 = f32[2,272]{1,0:T(2,128)} custom-call(f32[2,272]{1,0:T(2,128)} %get-tuple-element.34.x_ref), custom_call_target="tpu_custom_call" | custom-call | tf_op jit(solution)/shard_map/pallas_call | solution.py:102
  254.1 0.8 multiply_add_fusion
  254.9 0.7 fusion
  255.6 0.0 copy-start.16
  255.6 0.0 copy-start.8
  255.7 0.0 copy-start.14
  255.7 3.8 %add_convert_fusion = bf16[2304,272]{1,0:T(8,128)(2,1)} fusion(f32[2304,272]{1,0:T(8,128)} %get-tuple-element.33, bf16[2304,272]{1,0:T(8,128)(2,1)S(1)} %copy-done, f32[272]{0:T(512)S(1)} %get-tuple-element.46, f32[272]{0:T(512)S(1)} %get-tuple-element.45), kind=kLoop, calls=%fused_computation | loop fusion | flops 3133440 | bytes 5015680 | tf_op jit(solution)/shard_map/convert_element_type | solution.py:402
  259.5 0.6 pad_maximum_fusion.2
  260.2 0.1 pad_maximum_fusion
  260.2 0.6 reshape.32
  260.9 0.6 reshape.33
  (27 shorter events, 0.1 us)
Async XLA Ops:
  0.6 34.9 %copy-start.2 = (f32[2,68,1632]{2,0,1:T(2,128)S(1)}, f32[2,68,1632]{2,0,1:T(2,128)}, u32[]{:S(2)}) copy-start(f32[2,68,1632]{2,0,1:T(2,128)} %param.21) | copy-start | bytes 2663428
  0.6 34.1 %copy-start.3 = (f32[2,25,1632]{2,0,1:T(2,128)S(1)}, f32[2,25,1632]{2,0,1:T(2,128)}, u32[]{:S(2)}) copy-start(f32[2,25,1632]{2,0,1:T(2,128)} %param.18) | copy-start | bytes 979204
  0.7 38.6 %copy-start.1 = (bf16[2,1632,272]{1,2,0:T(8,128)(2,1)S(1)}, bf16[2,1632,272]{1,2,0:T(8,128)(2,1)}, u32[]{:S(2)}) copy-start(bf16[2,1632,272]{1,2,0:T(8,128)(2,1)} %param.23) | copy-start | bytes 5326852
  221.1 33.0 %copy-start.5 = (f32[2,272]{1,0:T(2,128)S(1)}, f32[2,272]{1,0:T(2,128)}, u32[]{:S(2)}) copy-start(f32[2,272]{1,0:T(2,128)} %v_ref.1) | copy-start | bytes 6532
  221.1 33.7 %copy-start.4 = (f32[2,272]{1,0:T(2,128)S(1)}, f32[2,272]{1,0:T(2,128)}, u32[]{:S(2)}) copy-start(f32[2,272]{1,0:T(2,128)} %om_ref.3) | copy-start | bytes 6532
  221.1 33.7 %copy-start.6 = (f32[2,272]{1,0:T(2,128)S(1)}, f32[2,272]{1,0:T(2,128)}, u32[]{:S(2)}) copy-start(f32[2,272]{1,0:T(2,128)} %g_ref.1) | copy-start | bytes 6532
  221.2 33.7 %copy-start.7 = (f32[2,272]{1,0:T(2,128)S(1)}, f32[2,272]{1,0:T(2,128)}, u32[]{:S(2)}) copy-start(f32[2,272]{1,0:T(2,128)} %b_ref.1) | copy-start | bytes 6532
  221.2 34.4 %copy-start = (bf16[2304,272]{1,0:T(8,128)(2,1)S(1)}, bf16[2304,272]{1,0:T(8,128)(2,1)}, u32[]{:S(2)}) copy-start(bf16[2304,272]{1,0:T(8,128)(2,1)} %get-tuple-element.29.x_ref) | copy-start | bytes 3760132
  255.6 3.9 %copy-start.16 = (f32[1,272]{1,0:T(1,128)S(1)}, f32[1,272]{1,0:T(1,128)}, u32[]{:S(2)}) copy-start(f32[1,272]{1,0:T(1,128)} %get-tuple-element.43) | copy-start | bytes 3268
  255.6 3.9 %copy-start.17 = (f32[1,272]{1,0:T(1,128)S(1)}, f32[1,272]{1,0:T(1,128)}, u32[]{:S(2)}) copy-start(f32[1,272]{1,0:T(1,128)} %get-tuple-element.44) | copy-start | bytes 3268
  255.6 4.5 %copy-start.8 = (f32[1,1632]{1,0:T(1,128)S(1)}, f32[1,1632]{1,0:T(1,128)}, u32[]{:S(2)}) copy-start(f32[1,1632]{1,0:T(1,128)} %get-tuple-element.35) | copy-start | bytes 19588
  255.7 4.5 %copy-start.9 = (f32[1,1632]{1,0:T(1,128)S(1)}, f32[1,1632]{1,0:T(1,128)}, u32[]{:S(2)}) copy-start(f32[1,1632]{1,0:T(1,128)} %get-tuple-element.39) | copy-start | bytes 19588
  255.7 4.5 %copy-start.10 = (f32[1,1632]{1,0:T(1,128)S(1)}, f32[1,1632]{1,0:T(1,128)}, u32[]{:S(2)}) copy-start(f32[1,1632]{1,0:T(1,128)} %get-tuple-element.36) | copy-start | bytes 19588
  255.7 4.5 %copy-start.11 = (f32[1,1632]{1,0:T(1,128)S(1)}, f32[1,1632]{1,0:T(1,128)}, u32[]{:S(2)}) copy-start(f32[1,1632]{1,0:T(1,128)} %get-tuple-element.40) | copy-start | bytes 19588
  255.7 4.5 %copy-start.12 = (f32[1,1632]{1,0:T(1,128)S(1)}, f32[1,1632]{1,0:T(1,128)}, u32[]{:S(2)}) copy-start(f32[1,1632]{1,0:T(1,128)} %get-tuple-element.37) | copy-start | bytes 19588
  255.7 4.5 %copy-start.13 = (f32[1,1632]{1,0:T(1,128)S(1)}, f32[1,1632]{1,0:T(1,128)}, u32[]{:S(2)}) copy-start(f32[1,1632]{1,0:T(1,128)} %get-tuple-element.41) | copy-start | bytes 19588
  255.7 4.5 %copy-start.14 = (f32[1,1632]{1,0:T(1,128)S(1)}, f32[1,1632]{1,0:T(1,128)}, u32[]{:S(2)}) copy-start(f32[1,1632]{1,0:T(1,128)} %get-tuple-element.38) | copy-start | bytes 19588
  255.7 4.5 %copy-start.15 = (f32[1,1632]{1,0:T(1,128)S(1)}, f32[1,1632]{1,0:T(1,128)}, u32[]{:S(2)}) copy-start(f32[1,1632]{1,0:T(1,128)} %get-tuple-element.42) | copy-start | bytes 19588

commit v2 on v1

--- a/solution.py
+++ b/solution.py
@@ -11,6 +11,8 @@
 REACH = KERN // 2
 LANES = 128
 WIDE = 2 * LANES
+SLOTS = 3
+TRANSPOSED = (((1,), (1,)), ((), ()))
 
 EPSILON = 0.001
 RATIO_MAX = 3.0
@@ -117,50 +119,49 @@
     )(stats)
 
 
-def expand_stats_kernel(chunk, x_ref, w_ref, mean_ref, stats_ref):
-    mean = mean_ref[0, 0:1, :]
-    weight = w_ref[0]
-
-    def body(step, carry):
-        rows = pl.ds(pl.multiple_of(step * chunk, chunk), chunk)
-        y = jnp.dot(x_ref[rows, :], weight, preferred_element_type=jnp.float32)
-        centered = y - mean
-        return carry[0] + fold_rows(centered), carry[1] + fold_rows(centered * centered)
-
-    zero = jnp.zeros((8, weight.shape[1]), jnp.float32)
-    first, second = lax.fori_loop(0, x_ref.shape[0] // chunk, body, (zero, zero))
-    stats_ref[0:1, :] = jnp.sum(first, axis=0, keepdims=True)
-    stats_ref[1:2, :] = jnp.sum(second, axis=0, keepdims=True)
+def expand_stats_kernel(layer, chunk, x_ref, w_ref, mean_ref, stats_ref):
+    mid = w_ref.shape[2]
+    for start in range(0, mid, WIDE):
+        stop = min(mid, start + WIDE)
+        mean = mean_ref[layer, 0:1, start:stop]
+
+        def body(step, carry):
+            rows = pl.ds(pl.multiple_of(step * chunk, chunk), chunk)
+            y = jnp.dot(x_ref[rows, :], w_ref[0, :, start:stop], preferred_element_type=jnp.float32)
+            centered = y - mean
+            return carry[0] + fold_rows(centered), carry[1] + fold_rows(centered * centered)
+
+        zero = jnp.zeros((8, stop - start), jnp.float32)
+        first, second = lax.fori_loop(0, x_ref.shape[0] // chunk, body, (zero, zero), unroll=4)
+        stats_ref[0:1, start:stop] = jnp.sum(first, axis=0, keepdims=True)
+        stats_ref[1:2, start:stop] = jnp.sum(second, axis=0, keepdims=True)
 
 
 def residual_kernel(
     layer, chunk, row_count, x_ref, p_ref, s_ref, m_ref, v_ref, g_ref, b_ref, w_ref, mean_ref,
     cur_ref, stats_ref, nm_ref, nv_ref,
 ):
-    @pl.when(pl.program_id(0) == 0)
-    def _():
-        pick = slice(layer, layer + 1)
-        scale, shift, new_mean, new_var = coefficients(
-            s_ref[0:1, :], s_ref[1:2, :], row_count,
-            m_ref[pick, :], v_ref[pick, :], g_ref[pick, :], b_ref[pick, :],
-        )
-        nm_ref[...] = new_mean
-        nv_ref[...] = new_var
-
-        def body(step, carry):
-            rows = pl.ds(pl.multiple_of(step * chunk, chunk), chunk)
-            cur_ref[rows, :] = (
-                x_ref[rows, :].astype(jnp.float32) + p_ref[rows, :] * scale + shift
-            ).astype(jnp.bfloat16)
-            return carry
-
-        lax.fori_loop(0, x_ref.shape[0] // chunk, body, 0)
-
-    expand_stats_kernel(chunk, cur_ref, w_ref, mean_ref, stats_ref)
+    pick = slice(layer - 1, layer)
+    scale, shift, new_mean, new_var = coefficients(
+        s_ref[0:1, :], s_ref[1:2, :], row_count,
+        m_ref[pick, :], v_ref[pick, :], g_ref[pick, :], b_ref[pick, :],
+    )
+    nm_ref[...] = new_mean
+    nv_ref[...] = new_var
+
+    def body(step, carry):
+        rows = pl.ds(pl.multiple_of(step * chunk, chunk), chunk)
+        cur_ref[rows, :] = (
+            x_ref[rows, :].astype(jnp.float32) + p_ref[rows, :] * scale + shift
+        ).astype(jnp.bfloat16)
+        return carry
+
+    lax.fori_loop(0, x_ref.shape[0] // chunk, body, 0, unroll=2)
+    expand_stats_kernel(layer, chunk, cur_ref, w_ref, mean_ref, stats_ref)
 
 
 def spread_kernel(
-    side, batch, row_count, blocks, x_ref, w_ref, dk_ref, sums_ref, mean_ref, var_ref, gain_ref, bias_ref,
+    layer, side, batch, row_count, blocks, x_ref, w_ref, dk_ref, sums_ref, mean_ref, var_ref, gain_ref, bias_ref,
     spread_ref, stats_ref, nm_ref, nv_ref, act, taps,
 ):
     chunk = side * batch
@@ -181,12 +182,12 @@
             act[half, step] = active[:, half * LANES : (half + 1) * LANES].reshape(side, batch, LANES)
         return carry
 
-    lax.fori_loop(0, side, activate, 0)
+    lax.fori_loop(0, side, activate, 0, unroll=4)
 
     def half_block(half, carry):
         lanes = pl.ds(pl.multiple_of(half * LANES, LANES), LANES)
         for tap in range(KERN * KERN):
-            taps[tap] = jnp.broadcast_to(dk_ref[0, tap : tap + 1, lanes], (8, LANES))
+            taps[tap] = jnp.broadcast_to(dk_ref[tap, layer : layer + 1, lanes], (8, LANES))
         mean = jnp.broadcast_to(mean_ref[0, 1:2, lanes], (8, LANES))
 
         def row(h, steps, sums):
@@ -241,43 +242,55 @@
     nv_ref[...] = new_var
     half_scale, half_shift = 0.5 * scale, 0.5 * shift
 
-    def lift(step, total):
-        rows = pl.ds(pl.multiple_of(step * chunk, chunk), chunk)
-        value = half_silu(v_ref[0, rows, :] * half_scale + half_shift)
-        lifted[block, rows, :] = value
-        return total + jnp.sum(value.reshape(side, batch, LANES), axis=0)
-
-    total = lax.fori_loop(0, side, lift, jnp.zeros((batch, LANES), jnp.float32))
-    pooled[:, pl.ds(pl.multiple_of(block * LANES, LANES), LANES)] = total / float(side * side)
+    for half in range(2):
+        lanes = slice(half * LANES, (half + 1) * LANES)
+
+        def lift(step, total):
+            rows = pl.ds(pl.multiple_of(step * chunk, chunk), chunk)
+            value = half_silu(v_ref[half, rows, :] * half_scale[:, lanes] + half_shift[:, lanes])
+            lifted[2 * block + half, rows, :] = value
+            return total + jnp.sum(value.reshape(side, batch, LANES), axis=0)
+
+        total = lax.fori_loop(0, side, lift, jnp.zeros((batch, LANES), jnp.float32), unroll=4)
+        start = pl.multiple_of((2 * block + half) * LANES, LANES)
+        pooled[:, pl.ds(start, LANES)] = total / float(side * side)
 
     @pl.when(block == blocks - 1)
     def _():
         pick = slice(layer, layer + 1)
-        squeezed = jnp.dot(
-            pooled[:, :mid], sw_ref[0], precision=lax.Precision.HIGHEST, preferred_element_type=jnp.float32
+        squeezed = lax.dot_general(
+            pooled[:, :mid], sw_ref[:, layer, :], TRANSPOSED,
+            precision=lax.Precision.HIGHEST, preferred_element_type=jnp.float32,
         )
         squeezed = half_silu(0.5 * (squeezed + sb_ref[pick, :]))
         grown = jnp.dot(
-            squeezed, ew_ref[0], precision=lax.Precision.HIGHEST, preferred_element_type=jnp.float32
+            squeezed, ew_ref[:, layer, :], precision=lax.Precision.HIGHEST, preferred_element_type=jnp.float32
         )
         gate[:, :mid] = 0.5 + 0.5 * jnp.tanh(0.5 * (grown + eb_ref[pick, :]))
         out_mean = om_ref[pick, :]
 
-        def project(step, sums):
+        def project(step, slot, sums):
             rows = pl.ds(pl.multiple_of(step * chunk, chunk), chunk)
             for index in range(pl.cdiv(mid, LANES)):
                 start = index * LANES
                 stop = min(mid, start + LANES)
                 value = lifted[index, rows, :].reshape(side, batch, LANES) * gate[:, start : start + LANES]
                 value = value.astype(jnp.bfloat16).reshape(chunk, LANES)
-                scaled[:, start:stop] = value[:, : stop - start]
-            product = jnp.dot(scaled[...], pw_ref[0], preferred_element_type=jnp.float32)
+                scaled[slot, :, start:stop] = value[:, : stop - start]
+            product = lax.dot_general(
+                scaled[slot], pw_ref[0], TRANSPOSED, preferred_element_type=jnp.float32
+            )
             proj_ref[rows, :] = product
             centered = product - out_mean
             return sums[0] + fold_rows(centered), sums[1] + fold_rows(centered * centered)
 
+        def project_group(group, sums):
+            for slot in range(SLOTS):
+                sums = project(group * SLOTS + slot, slot, sums)
+            return sums
+
         zero = jnp.zeros((8, proj_ref.shape[1]), jnp.float32)
-        first, second = lax.fori_loop(0, side, project, (zero, zero))
+        first, second = lax.fori_loop(0, side // SLOTS, project_group, (zero, zero))
         stats_ref[0:1, :] = jnp.sum(first, axis=0, keepdims=True)
         stats_ref[1:2, :] = jnp.sum(second, axis=0, keepdims=True)
 
@@ -326,24 +339,25 @@
     means, variances, out_means, out_vars = [], [], [], []
     for layer in range(layers):
         wide_params = [layer_columns(2, WIDE, layer)] * 4
+        depth_spec = pl.BlockSpec((taps_count, layers, WIDE), lambda j: (0, 0, j))
         weight_spec = layer_columns(out, WIDE, layer)
         if layer == 0:
             stats = pl.pallas_call(
-                functools.partial(expand_stats_kernel, chunk),
-                grid=(wide_steps,),
-                in_specs=[whole((rows, out)), weight_spec, wide_params[0]],
-                out_specs=columns(2, WIDE),
+                functools.partial(expand_stats_kernel, layer, chunk),
+                grid=(1,),
+                in_specs=[whole((rows, out)), of_layer(expand_weight.shape, layer), whole(mid_mean.shape)],
+                out_specs=whole((2, mid)),
                 out_shape=f32(2, mid),
                 compiler_params=PARAMS,
             )(current, expand_weight, mid_mean)
         else:
             current, stats, new_mean, new_var = pl.pallas_call(
-                functools.partial(residual_kernel, layer - 1, chunk, row_count),
-                grid=(wide_steps,),
+                functools.partial(residual_kernel, layer, chunk, row_count),
+                grid=(1,),
                 in_specs=[whole((rows, out)), whole((rows, out)), whole((2, out))]
                 + [whole((layers, out))] * 4
-                + [weight_spec, wide_params[0]],
-                out_specs=[whole((rows, out)), columns(2, WIDE), whole((1, out)), whole((1, out))],
+                + [of_layer(expand_weight.shape, layer), whole(mid_mean.shape)],
+                out_specs=[whole((rows, out)), whole((2, mid)), whole((1, out)), whole((1, out))],
                 out_shape=[jax.ShapeDtypeStruct((rows, out), jnp.bfloat16), f32(2, mid), f32(1, out), f32(1, out)],
                 compiler_params=PARAMS,
             )(current, projected, out_sums, out_mean, out_var, out_gain, out_bias, expand_weight, mid_mean)
@@ -351,9 +365,9 @@
             out_vars.append(new_var)
         sums = all_sum(stats, n_row, n_col, 1)
         spread, stats, mean_a, var_a = pl.pallas_call(
-            functools.partial(spread_kernel, side, batch, row_count, blocks),
+            functools.partial(spread_kernel, layer, side, batch, row_count, blocks),
             grid=(wide_steps,),
-            in_specs=[whole((rows, out)), weight_spec, layer_columns(taps_count, WIDE, layer), columns(2, WIDE)]
+            in_specs=[whole((rows, out)), weight_spec, depth_spec, columns(2, WIDE)]
             + wide_params,
             out_specs=[
                 pl.BlockSpec((2, rows, LANES), lambda j: (j, 0, 0)),
@@ -365,30 +379,31 @@
                 pltpu.VMEM((taps_count, 8, LANES), jnp.float32),
             ],
             compiler_params=PARAMS,
-        )(current, expand_weight, depth_kernel, sums, mid_mean, mid_var, mid_gain, mid_bias)
+        )(current, expand_weight, depth_kernel.transpose(1, 0, 2), sums, mid_mean, mid_var, mid_gain, mid_bias)
         sums = all_sum(stats, n_row, n_col, 1)
         projected, stats, mean_b, var_b = pl.pallas_call(
             functools.partial(lift_kernel, layer, side, batch, row_count, mid),
-            grid=(blocks,),
-            in_specs=[pl.BlockSpec((1, rows, LANES), lambda j: (j, 0, 0)), columns(2, LANES)]
-            + [layer_columns(2, LANES, layer)] * 4
+            grid=(wide_steps,),
+            in_specs=[pl.BlockSpec((2, rows, LANES), lambda j: (j, 0, 0)), columns(2, WIDE)]
+            + wide_params
             + [
-                of_layer(squeeze_weight.shape, layer), whole(squeeze_bias.shape),
-                of_layer(excite_weight.shape, layer), whole(excite_bias.shape),
-                of_layer(project_weight.shape, layer), whole(out_mean.shape),
+                whole((squeeze, layers, mid)), whole(squeeze_bias.shape),
+                whole((squeeze, layers, mid)), whole(excite_bias.shape),
+                of_layer((layers, out, mid), layer), whole(out_mean.shape),
             ],
-            out_specs=[whole((rows, out)), whole((2, out)), columns(1, LANES), columns(1, LANES)],
+            out_specs=[whole((rows, out)), whole((2, out)), columns(1, WIDE), columns(1, WIDE)],
             out_shape=[f32(rows, out), f32(2, out), f32(1, mid), f32(1, mid)],
             scratch_shapes=[
-                pltpu.VMEM((blocks, rows, LANES), jnp.float32),
-                pltpu.VMEM((batch, blocks * LANES), jnp.float32),
-                pltpu.VMEM((batch, blocks * LANES), jnp.float32),
-                pltpu.VMEM((chunk, mid), jnp.bfloat16),
+                pltpu.VMEM((2 * wide_steps, rows, LANES), jnp.float32),
+                pltpu.VMEM((batch, wide_steps * WIDE), jnp.float32),
+                pltpu.VMEM((batch, wide_steps * WIDE), jnp.float32),
+                pltpu.VMEM((SLOTS, chunk, mid), jnp.bfloat16),
             ],
             compiler_params=PARAMS,
         )(
             spread, sums, mid_mean, mid_var, mid_gain, mid_bias,
-            squeeze_weight, squeeze_bias, excite_weight, excite_bias, project_weight, out_mean,
+            squeeze_weight.transpose(2, 0, 1), squeeze_bias, excite_weight.transpose(1, 0, 2), excite_bias,
+            project_weight.transpose(0, 2, 1), out_mean,
         )
         out_sums = all_sum(stats, n_row, n_col, 2)
         means += [mean_a, mean_b]

time: 262 us -> 208 us (0.79)
  Pallas kernels: 246 us -> 199 us
  local copies, waits for them, and re-layouts: 8.54 us -> 1.35 us
    pallas_call x4, Pallas kernels: 134 us -> 93.2 us  [the longest x2 71 us: per_device(): pl.pallas_call(functools.partial(spread_kernel, layer, side, batch, row_c...]
    unnamed x40 -> x30, local copies, waits for them, and re-layouts: 7.27 us -> 0.08 us
    pallas_call x2, Pallas kernels: 44 us -> 38.1 us  [per_device(): pl.pallas_call(functools.partial(lift_kernel, layer, side, batch, row_cou...]
where the time goes in v2:
time: 208 us; the launch traced here: 207 us
  Pallas kernels  199 us (96%)
  other arithmetic  5.93 us (3%)
    pallas_call x2, Pallas kernels, per_device(): pl.pallas_call(functools.partial(spread_kernel, layer, side, batch, row_c...  71 us
    pallas_call x6, Pallas kernels, all_sum(): pl.pallas_call(functools.partial(exchange_kernel, n_row, n_col), out_shap...  68 us
    pallas_call x2, Pallas kernels, per_device(): pl.pallas_call(functools.partial(lift_kernel, layer, side, batch, row_cou...  38.1 us
    pallas_call x1, Pallas kernels, per_device(): pl.pallas_call(functools.partial(residual_kernel, layer, chunk, row_count...  12.1 us
    pallas_call x1, Pallas kernels, per_device(): pl.pallas_call(functools.partial(expand_stats_kernel, layer, chunk), grid...  10.1 us

profile of v2, /device:TPU:0, one launch (start us, length us, event | category | flops | bytes accessed | tf_op | source)
XLA Modules:
  0.0 207.4 jit_solution(9022703813932211089)
XLA Ops:
  0.6 10.1 %shard_map.191.x_ref = f32[2,1632]{1,0:T(2,128)} custom-call(bf16[2304,272]{1,0:T(8,128)(2,1)} %bitcast.14, bf16[2,272,1632]{2,1,0:T(8,128)(2,1)} %w_ref.7, f32[2,2,1632]{2,1,0:T(2,128)} %mean_ref.11), custom_call_target="tpu_custom_call" | custom-call | tf_op jit(solution)/shard_map/pallas_call | solution.py:345
  10.7 13.7 %shard_map.192.sums_ref = f32[2,1632]{1,0:T(2,128)} custom-call(f32[2,1632]{1,0:T(2,128)} %shard_map.191.x_ref), custom_call_target="tpu_custom_call" | custom-call | tf_op jit(solution)/shard_map/pallas_call | solution.py:104
  24.4 35.5 %shard_map.193 = (f32[14,2304,128]{2,1,0:T(8,128)}, f32[2,1632]{1,0:T(2,128)}, f32[1,1632]{1,0:T(1,128)}, f32[1,1632]{1,0:T(1,128)}) custom-call(bf16[2304,272]{1,0:T(8,128)(2,1)} %bitcast.15, bf16[2,272,1632]{2,1,0:T(8,128)(2,1)} %w_ref.7, f32[25,2,1632]{2,1,0:T(2,128)} %bitcast.24, f32[2,1632]{1,0:T(2,128)} %shard_map.192.sums_ref, ...), custom_call_target="tpu_custom_call" | custom-call | tf_op jit(solution)/shard_map/pallas_call | solution.py:367
  59.9 11.2 %shard_map.194.sums_ref = f32[2,1632]{1,0:T(2,128)} custom-call(f32[2,1632]{1,0:T(2,128)} %get-tuple-element.26.x_ref), custom_call_target="tpu_custom_call" | custom-call | tf_op jit(solution)/shard_map/pallas_call | solution.py:104
  71.1 18.9 %shard_map.195 = (f32[2304,272]{1,0:T(8,128)}, f32[2,272]{1,0:T(2,128)}, f32[1,1632]{1,0:T(1,128)}, f32[1,1632]{1,0:T(1,128)}) custom-call(f32[14,2304,128]{2,1,0:T(8,128)} %get-tuple-element.25.v_ref, f32[2,1632]{1,0:T(2,128)} %shard_map.194.sums_ref, f32[2,2,1632]{2,1,0:T(2,128)} %mean_ref.11, f32[2,2,1632]{2,1,0:T(2,128)} %var_ref.7, ...), custom_call_target="tpu_custom_call" | custom-call | tf_op jit(solution)/shard_map/pallas_call | solution.py:384
  90.1 10.2 %shard_map.196.s_ref = f32[2,272]{1,0:T(2,128)} custom-call(f32[2,272]{1,0:T(2,128)} %get-tuple-element.28.x_ref), custom_call_target="tpu_custom_call" | custom-call | tf_op jit(solution)/shard_map/pallas_call | solution.py:104
  100.3 12.1 %shard_map.197 = (bf16[2304,272]{1,0:T(8,128)(2,1)}, f32[2,1632]{1,0:T(2,128)}, f32[1,272]{1,0:T(1,128)}, f32[1,272]{1,0:T(1,128)}) custom-call(bf16[2304,272]{1,0:T(8,128)(2,1)} %bitcast.16, f32[2304,272]{1,0:T(8,128)} %get-tuple-element.27.p_ref, f32[2,272]{1,0:T(2,128)} %shard_map.196.s_ref, f32[2,272]{1,0:T(2,128)} %om_ref.3, f32[2,272]{1,0:T(2,128)} %v_ref.1, ...), custom_call_target="tpu_custom_call" | custom-call | tf_op jit(solution)/shard_map/pallas_call | solution.py:354
  112.3 11.2 %shard_map.198.sums_ref = f32[2,1632]{1,0:T(2,128)} custom-call(f32[2,1632]{1,0:T(2,128)} %get-tuple-element.30.x_ref), custom_call_target="tpu_custom_call" | custom-call | tf_op jit(solution)/shard_map/pallas_call | solution.py:104
  123.5 35.5 %shard_map.199 = (f32[14,2304,128]{2,1,0:T(8,128)}, f32[2,1632]{1,0:T(2,128)}, f32[1,1632]{1,0:T(1,128)}, f32[1,1632]{1,0:T(1,128)}) custom-call(bf16[2304,272]{1,0:T(8,128)(2,1)} %get-tuple-element.29.x_ref, bf16[2,272,1632]{2,1,0:T(8,128)(2,1)} %w_ref.7, f32[25,2,1632]{2,1,0:T(2,128)} %bitcast.25, f32[2,1632]{1,0:T(2,128)} %shard_map.198.sums_ref, ...), custom_call_target="tpu_custom_call" | custom-call | tf_op jit(solution)/shard_map/pallas_call | solution.py:367
  159.0 10.9 %shard_map.200.sums_ref = f32[2,1632]{1,0:T(2,128)} custom-call(f32[2,1632]{1,0:T(2,128)} %get-tuple-element.32.x_ref), custom_call_target="tpu_custom_call" | custom-call | tf_op jit(solution)/shard_map/pallas_call | solution.py:104
  169.9 0.0 copy-start.2
  169.9 0.0 copy-start.1
  169.9 0.0 copy-start.3
  169.9 0.0 copy-start.4
  169.9 0.0 copy-start
  169.9 19.1 %shard_map.201 = (f32[2304,272]{1,0:T(8,128)}, f32[2,272]{1,0:T(2,128)}, f32[1,1632]{1,0:T(1,128)}, f32[1,1632]{1,0:T(1,128)}) custom-call(f32[14,2304,128]{2,1,0:T(8,128)} %get-tuple-element.31.v_ref, f32[2,1632]{1,0:T(2,128)} %shard_map.200.sums_ref, f32[2,2,1632]{2,1,0:T(2,128)} %mean_ref.11, f32[2,2,1632]{2,1,0:T(2,128)} %var_ref.7, ...), custom_call_target="tpu_custom_call" | custom-call | tf_op jit(solution)/shard_map/pallas_call | solution.py:384
  189.1 10.9 %shard_map.202 = f32[2,272]{1,0:T(2,128)} custom-call(f32[2,272]{1,0:T(2,128)} %get-tuple-element.34.x_ref), custom_call_target="tpu_custom_call" | custom-call | tf_op jit(solution)/shard_map/pallas_call | solution.py:104
  200.0 0.0 copy-done.2
  200.0 0.8 multiply_add_fusion
  200.8 0.0 copy-done.3
  200.8 0.7 fusion
  201.5 0.0 copy-done
  201.6 0.0 copy-start.13
  201.6 0.0 copy-start.5
  201.6 0.0 copy-start.6
  201.6 0.0 copy-start.7
  201.6 0.0 copy-start.11
  201.7 3.8 %add_convert_fusion = bf16[2304,272]{1,0:T(8,128)(2,1)} fusion(f32[2304,272]{1,0:T(8,128)} %get-tuple-element.33, bf16[2304,272]{1,0:T(8,128)(2,1)S(1)} %copy-done, f32[272]{0:T(512)S(1)} %get-tuple-element.46, f32[272]{0:T(512)S(1)} %get-tuple-element.45), kind=kLoop, calls=%fused_computation | loop fusion | flops 3133440 | bytes 5015680 | tf_op jit(solution)/shard_map/convert_element_type | solution.py:417
  205.5 0.6 pad_maximum_fusion.2
  206.1 0.1 pad_maximum_fusion
  206.2 0.6 reshape.32
  206.8 0.6 reshape.33
  (17 shorter events, 0.0 us)
Async XLA Ops:
  169.9 30.1 %copy-start.2 = (f32[2,272]{1,0:T(2,128)S(1)}, f32[2,272]{1,0:T(2,128)}, u32[]{:S(2)}) copy-start(f32[2,272]{1,0:T(2,128)} %v_ref.1) | copy-start | bytes 6532
  169.9 30.9 %copy-start.1 = (f32[2,272]{1,0:T(2,128)S(1)}, f32[2,272]{1,0:T(2,128)}, u32[]{:S(2)}) copy-start(f32[2,272]{1,0:T(2,128)} %om_ref.3) | copy-start | bytes 6532
  169.9 30.9 %copy-start.3 = (f32[2,272]{1,0:T(2,128)S(1)}, f32[2,272]{1,0:T(2,128)}, u32[]{:S(2)}) copy-start(f32[2,272]{1,0:T(2,128)} %g_ref.1) | copy-start | bytes 6532
  169.9 30.9 %copy-start.4 = (f32[2,272]{1,0:T(2,128)S(1)}, f32[2,272]{1,0:T(2,128)}, u32[]{:S(2)}) copy-start(f32[2,272]{1,0:T(2,128)} %b_ref.1) | copy-start | bytes 6532
  169.9 31.6 %copy-start = (bf16[2304,272]{1,0:T(8,128)(2,1)S(1)}, bf16[2304,272]{1,0:T(8,128)(2,1)}, u32[]{:S(2)}) copy-start(bf16[2304,272]{1,0:T(8,128)(2,1)} %get-tuple-element.29.x_ref) | copy-start | bytes 3760132
  201.6 3.9 %copy-start.13 = (f32[1,272]{1,0:T(1,128)S(1)}, f32[1,272]{1,0:T(1,128)}, u32[]{:S(2)}) copy-start(f32[1,272]{1,0:T(1,128)} %get-tuple-element.43) | copy-start | bytes 3268
  201.6 3.9 %copy-start.14 = (f32[1,272]{1,0:T(1,128)S(1)}, f32[1,272]{1,0:T(1,128)}, u32[]{:S(2)}) copy-start(f32[1,272]{1,0:T(1,128)} %get-tuple-element.44) | copy-start | bytes 3268
  201.6 4.5 %copy-start.5 = (f32[1,1632]{1,0:T(1,128)S(1)}, f32[1,1632]{1,0:T(1,128)}, u32[]{:S(2)}) copy-start(f32[1,1632]{1,0:T(1,128)} %get-tuple-element.35) | copy-start | bytes 19588
  201.6 4.5 %copy-start.6 = (f32[1,1632]{1,0:T(1,128)S(1)}, f32[1,1632]{1,0:T(1,128)}, u32[]{:S(2)}) copy-start(f32[1,1632]{1,0:T(1,128)} %get-tuple-element.39) | copy-start | bytes 19588
  201.6 4.5 %copy-start.7 = (f32[1,1632]{1,0:T(1,128)S(1)}, f32[1,1632]{1,0:T(1,128)}, u32[]{:S(2)}) copy-start(f32[1,1632]{1,0:T(1,128)} %get-tuple-element.36) | copy-start | bytes 19588
  201.6 4.5 %copy-start.8 = (f32[1,1632]{1,0:T(1,128)S(1)}, f32[1,1632]{1,0:T(1,128)}, u32[]{:S(2)}) copy-start(f32[1,1632]{1,0:T(1,128)} %get-tuple-element.40) | copy-start | bytes 19588
  201.6 4.5 %copy-start.9 = (f32[1,1632]{1,0:T(1,128)S(1)}, f32[1,1632]{1,0:T(1,128)}, u32[]{:S(2)}) copy-start(f32[1,1632]{1,0:T(1,128)} %get-tuple-element.37) | copy-start | bytes 19588
  201.6 4.5 %copy-start.10 = (f32[1,1632]{1,0:T(1,128)S(1)}, f32[1,1632]{1,0:T(1,128)}, u32[]{:S(2)}) copy-start(f32[1,1632]{1,0:T(1,128)} %get-tuple-element.41) | copy-start | bytes 19588
  201.6 4.5 %copy-start.11 = (f32[1,1632]{1,0:T(1,128)S(1)}, f32[1,1632]{1,0:T(1,128)}, u32[]{:S(2)}) copy-start(f32[1,1632]{1,0:T(1,128)} %get-tuple-element.38) | copy-start | bytes 19588
  201.7 4.5 %copy-start.12 = (f32[1,1632]{1,0:T(1,128)S(1)}, f32[1,1632]{1,0:T(1,128)}, u32[]{:S(2)}) copy-start(f32[1,1632]{1,0:T(1,128)} %get-tuple-element.42) | copy-start | bytes 19588
